TPU v7x, 256 devices: a whole 4x4x8 slice. The times are simulated.
256 devices in a mesh: dp: 64 (over z, y, core), mp: 4 (over x).
Axes of the slice: x: 4, y: 4, z: 8, core: 2. Of those that a mesh axis runs over, the one named last changes fastest.
Arguments:
- hidden: bfloat16 [128, 64, 3584], P('dp', None, 'mp'), may hold values from -6 to 6
- rewards: float32 [128, 64], P('dp'), may hold values from -6 to 6
- actions: int32 [128, 64], P('dp'), may hold values from 0 to 152063, as said below
- lengths: int32 [128], P('dp'), may hold values from 1 to 64, 4096 in all
- table: bfloat16 [152064, 3584], P('dp', 'mp'), may hold values from -0.09375 to 0.09375
- q_one: bfloat16 [3584, 3584], P('dp', 'mp'), may hold values from -0.09375 to 0.09375
- q_two: bfloat16 [3584, 3584], P('dp', 'mp'), may hold values from -0.09375 to 0.09375
- t_one: bfloat16 [3584, 3584], P('dp', 'mp'), may hold values from -0.09375 to 0.09375
- t_two: bfloat16 [3584, 3584], P('dp', 'mp'), may hold values from -0.09375 to 0.09375
- value_weight: bfloat16 [3584], P('mp'), may hold values from -0.09375 to 0.09375
- value_bias: float32 [1], replicated, may hold values from -3 to 3
Outputs:
- loss: float32 [], replicated
- grad_q_one: float32 [3584, 3584], P('dp', 'mp')
- grad_q_two: float32 [3584, 3584], P('dp', 'mp')
- grad_value: float32 [3584], P('mp')
- grad_bias: float32 [1], replicated
- target_one: bfloat16 [3584, 3584], P('dp', 'mp')
- target_two: bfloat16 [3584, 3584], P('dp', 'mp')
Inputs may be any that keep to these rules, and one draw needn't show every extreme that they name: `actions`: among the 128 positions of the prompts of one index of dp, exactly 2 action ids fall in each of the aligned blocks of 2376 vocabulary rows.
All inputs are finite; a program needn't handle non-finite values. No bound on the sum of `lengths` on one device may be relied on, other than what follows from the above.
Results may differ from a plain program's by a relative error of at most 0.0045.
Values may be sent and summed in bfloat16 or wider, within the bound.
No kernel may reach another device: no remote copies, remote signals or barrier semaphores. Data moves between devices by JAX's collectives and lax.ppermute only.
A program may use at most 192 MiB of HBM per device.

v0:
```python
import jax
import jax.numpy as jnp
from jax import lax
from jax.sharding import PartitionSpec as P

discount = 0.99
expectile = 0.7
polyak_rate = 0.005


def joined_along(pieces, dim):
    dims = list(pieces.shape[1:])
    dims[dim] *= pieces.shape[0]
    return jnp.moveaxis(pieces, 0, dim).reshape(dims)


def sent_to_all(shard, axis):
    copies = jnp.broadcast_to(shard, (lax.axis_size(axis), *shard.shape))
    return lax.all_to_all(copies, axis, split_axis=0, concat_axis=0, tiled=True)


def collect(shard, axis, dim):
    return joined_along(sent_to_all(shard, axis), dim)


def side_by_side(arrays, axis, dim, along):
    both = jnp.concatenate(arrays, axis=along)
    whole, at, finished = (lax.all_gather(both, axis, axis=dim, tiled=True), 0, [])
    for a in arrays:
        finished.append(lax.slice_in_dim(whole, at, at + a.shape[along], axis=along))
        at += a.shape[along]
    return tuple(finished)


def of_everyone(shard, axis):
    everything = sent_to_all(shard, axis)
    return jnp.sum(everything, axis=0)


def packed_total(arrays, axis):
    ravelled, at, finished = (jnp.concatenate([a.reshape(-1) for a in arrays]), 0, [])
    subtotal = of_everyone(ravelled, axis)
    for a in arrays:
        finished.append(subtotal[at : at + a.size].reshape(a.shape))
        at += a.size
    return tuple(finished)


def head_gelu(inputs):
    return jax.nn.gelu(inputs, approximate=True)


def slope(preact, upstream):
    _, pullback = jax.vjp(head_gelu, preact)
    return pullback(upstream)[0]


def critic_terms(q_first, q_second, t_first, t_second, values, rewards, lengths):
    positions = jnp.arange(values.shape[1], dtype=jnp.int32)[None, :]
    valid = positions < lengths[:, None]
    follows = positions + 1 < lengths[:, None]
    shifted = jnp.concatenate([values[:, 1:], jnp.zeros_like(values[:, :1])], axis=1)
    target = rewards + discount * jnp.where(follows, shifted, 0.0)
    lowest = jnp.minimum(t_first, t_second)
    spread = lowest - values
    weights = jnp.where(spread < 0.0, 1.0 - expectile, expectile)
    err_one = q_first - target
    err_two = q_second - target
    loss_sum = jnp.sum(
        jnp.where(valid, err_one * err_one + err_two * err_two + weights * spread * spread, 0.0)
    )
    grad_first = jnp.where(valid, 2.0 * err_one, 0.0)
    grad_second = jnp.where(valid, 2.0 * err_two, 0.0)
    grad_values = jnp.where(valid, -2.0 * weights * spread, 0.0)
    return (grad_first, grad_second, grad_values, loss_sum)


def lookup(wanted_ids, table):
    holders_count = lax.axis_size("dp")
    local_rows = table.shape[0]
    id_count = wanted_ids.shape[0]
    per_holder = id_count // holders_count
    holders = wanted_ids // local_rows
    ranking = jnp.argsort(holders * id_count + jnp.arange(id_count, dtype=jnp.int32))
    requests = (wanted_ids % local_rows)[ranking].reshape(holders_count, per_holder)
    found = table[lax.all_to_all(requests, "dp", split_axis=0, concat_axis=0, tiled=True)]
    fetched = lax.all_to_all(found, "dp", split_axis=0, concat_axis=0, tiled=True)
    inverse = jnp.argsort(ranking)
    return fetched.reshape(id_count, -1)[inverse]


def on_device(
    hidden, rewards, actions, lengths, table, q_one, q_two, t_one, t_two, value_weight, value_bias
):
    prompt_count, slot_count, local_width = hidden.shape
    positions_count = prompt_count * slot_count
    gathered = collect(hidden, "mp", 2)
    flat = gathered.reshape(positions_count, -1)
    local_flat = hidden.reshape(positions_count, local_width)
    embed = lookup(actions.reshape(positions_count), table).astype(jnp.float32)
    head_cols = q_one.shape[1]

    def add_rows(pieces):
        return tuple((jnp.dot(flat, piece, preferred_element_type=jnp.float32) for piece in pieces))

    preacts = add_rows(side_by_side((q_one, q_two, t_one, t_two), "dp", 0, 1))
    partial_value = [jnp.sum(head_gelu(preact) * embed, axis=1) for preact in preacts]
    value_part = jnp.dot(local_flat, value_weight, preferred_element_type=jnp.float32)
    summed = packed_total(
        (partial_value[0], partial_value[1], partial_value[2], partial_value[3], value_part), "mp"
    )
    shaped = [piece.reshape(prompt_count, slot_count) for piece in summed]
    values = shaped[4] + value_bias[0]
    grad_first, grad_second, grad_values, loss_sum = critic_terms(
        shaped[0], shaped[1], shaped[2], shaped[3], values, rewards, lengths
    )
    back_one = slope(preacts[0], grad_first.reshape(-1, 1) * embed).astype(jnp.bfloat16)
    back_two = slope(preacts[1], grad_second.reshape(-1, 1) * embed).astype(jnp.bfloat16)
    local_count = jnp.sum(lengths).astype(jnp.float32)
    holders_count = lax.axis_size("dp")
    row_share = q_one.shape[0]
    dims = (((0,), (0,)), ((), ()))
    total_count = of_everyone(local_count, "dp")
    factor = 1.0 / total_count
    term_one = (
        lax.dot_general(flat, back_one, dims, preferred_element_type=jnp.float32) * factor
    ).reshape(holders_count, row_share, head_cols)
    term_two = (
        lax.dot_general(flat, back_two, dims, preferred_element_type=jnp.float32) * factor
    ).reshape(holders_count, row_share, head_cols)
    head_one = jnp.sum(
        lax.all_to_all(
            term_one.astype(jnp.bfloat16), "dp", split_axis=0, concat_axis=0, tiled=True
        ).astype(term_one.dtype),
        axis=0,
    )
    head_two = jnp.sum(
        lax.all_to_all(
            term_two.astype(jnp.bfloat16), "dp", split_axis=0, concat_axis=0, tiled=True
        ).astype(term_two.dtype),
        axis=0,
    )
    value_part_grad = jnp.dot(
        grad_values.reshape(-1), local_flat.astype(jnp.float32), precision=lax.Precision.HIGHEST
    )
    bias_part = jnp.sum(grad_values)
    value_grad, bias_grad, loss_total = packed_total(
        (value_part_grad * factor, bias_part * factor, loss_sum * factor), "dp"
    )
    new_one = (
        (1.0 - polyak_rate) * t_one.astype(jnp.float32) + polyak_rate * q_one.astype(jnp.float32)
    ).astype(jnp.bfloat16)
    new_two = (
        (1.0 - polyak_rate) * t_two.astype(jnp.float32) + polyak_rate * q_two.astype(jnp.float32)
    ).astype(jnp.bfloat16)
    return (loss_total, head_one, head_two, value_grad, bias_grad.reshape(1), new_one, new_two)


def solution(mesh):
    in_specs = (
        P("dp", None, "mp"),
        P("dp", None),
        P("dp", None),
        P("dp"),
        P("dp", "mp"),
        P("dp", "mp"),
        P("dp", "mp"),
        P("dp", "mp"),
        P("dp", "mp"),
        P("mp"),
        P(),
    )
    out_specs = (P(), P("dp", "mp"), P("dp", "mp"), P("mp"), P(), P("dp", "mp"), P("dp", "mp"))
    return jax.shard_map(
        on_device, mesh=mesh, in_specs=in_specs, out_specs=out_specs, check_vma=False
    )
```

profile of v0, /device:TPU:8, one launch (start us, length us, event | category | flops | bytes accessed | tf_op | source)
XLA Modules:
  0.0 505.3 jit_solution(7394394523861316911)
XLA Ops:
  7.2 1.9 pad_maximum_fusion
  10.8 2.5 sort.31
  13.3 1.2 gather_fusion
  14.7 20.6 %all_to_all.50 = s32[64,1,2]{2,1,0:T(1,128)S(1)} all-to-all(s32[64,1,2]{2,1,0:T(1,128)S(1)} %bitcast.68), channel_id=1, replica_groups=mesh['dp'=64,'mp'=4] {'dp'}, dimensions={0} | all-to-all | bytes 1024 | tf_op jit(solution)/shard_map/all_to_all | solution.py:86
  35.6 3.8 gather_fusion.1
  39.5 18.6 %all_to_all.51 = bf16[64,2,896]{2,1,0:T(2,128)(2,1)S(1)} all-to-all(bf16[64,2,896]{2,1,0:T(2,128)(2,1)S(1)} %reshape.178), channel_id=1, replica_groups=mesh['dp'=64,'mp'=4] {'dp'}, dimensions={0} | all-to-all | bytes 458752 | tf_op jit(solution)/shard_map/all_to_all | solution.py:87
  58.1 2.1 broadcast_in_dim.36
  60.1 4.3 all-to-all-start
  64.4 2.5 sort.32
  68.6 0.9 gather_fusion.2
  69.6 8.9 %all-to-all-done = bf16[4,2,64,896]{3,2,1,0:T(8,128)(2,1)S(1)} async-done(((bf16[4,2,64,896]{3,2,1,0:T(8,128)(2,1)}), bf16[4,2,64,896]{3,2,1,0:T(8,128)(2,1)S(1)}, u32[]{:S(2)}, u32[]{:S(2)}) %all-to-all-start) | async-done | bytes 917536 | tf_op jit(solution)/shard_map/all_to_all | solution.py:19
  79.1 5.1 %all-to-all-start.4 = ((f32[64,1,1]{2,1,0:T(1,128)}), f32[64,1,1]{2,1,0:T(1,128)S(1)}, u32[]{:S(2)}, u32[]{:S(2)}) async-start(f32[64,1,1]{2,1,0:T(1,128)} %broadcast_in_dim.42), calls=%async_computation.4 | async-start | bytes 65536 | tf_op jit(solution)/shard_map/all_to_all | solution.py:19
  85.1 53.0 %all-gather.2.cloned.1.call-done = bf16[3584,3584]{1,0:T(8,128)(2,1)} async-done(((bf16[56,3584]{1,0:T(8,128)(2,1)}), bf16[3584,3584]{1,0:T(8,128)(2,1)}) %all-gather.2.cloned.1.call-update) | async-done | bytes 25690128 | tf_op jit(solution)/shard_map/all_gather | solution.py:28
  138.0 4.8 fusion.10
  142.9 5.5 %fusion.75 = (f32[128]{0:T(128)S(1)}, f32[128]{0:T(128)S(1)}, f32[128,896]{0,1:T(8,128)S(1)}) fusion(bf16[128,896]{0,1:T(8,128)(2,1)S(1)} %copy.44, f32[128,896]{0,1:T(8,128)S(1)} %fusion.10, bf16[128,3584]{1,0:T(8,128)(2,1)S(1)} %bitcast.63, bf16[3584,3584]{1,0:T(8,128)(2,1)} %all-gather.2.cloned.1.call-done), kind=kOutput, calls=%fused_computation.76 | convolution fusion | flops 824491776 | bytes 8487936 | tf_op jit(solution)/shard_map/dot_general | solution.py:104
  148.4 1.6 copy-done.9
  150.1 1.9 fusion.57
  152.0 1.9 fusion.71
  154.5 4.2 all-to-all-start.3
  160.8 3.3 all-to-all-done.3
  167.0 0.8 broadcast_in_dim.43
  167.8 7.5 %all-to-all-start.5 = ((f32[64,1,898]{2,1,0:T(1,128)}), f32[64,1,898]{2,1,0:T(1,128)S(1)}, u32[]{:S(2)}, u32[]{:S(2)}) async-start(f32[64,1,898]{2,1,0:T(1,128)} %broadcast_in_dim.43), calls=%async_computation.5 | async-start | bytes 524288 | tf_op jit(solution)/shard_map/all_to_all | solution.py:19
  175.4 4.7 fusion.9
  180.2 9.6 %copy.49 = bf16[3584,896]{1,0:T(8,128)(2,1)} copy(bf16[3584,896]{0,1:T(8,128)(2,1)} %fusion.9) | data formatting | bytes 12845056 | tf_op jit(solution)/shard_map/convert_element_type | solution.py:139
  189.7 10.5 %all-to-all-start.7 = ((bf16[64,56,896]{2,1,0:T(8,128)(2,1)}), bf16[64,56,896]{2,1,0:T(8,128)(2,1)}, u32[]{:S(2)}, u32[]{:S(2)}) async-start(bf16[64,56,896]{2,1,0:T(8,128)(2,1)} %bitcast.57), calls=%async_computation.7 | async-start | bytes 12845056 | tf_op jit(solution)/shard_map/all_to_all | solution.py:138
  200.3 4.7 fusion.8
  205.0 9.4 %copy.48 = bf16[3584,896]{1,0:T(8,128)(2,1)} copy(bf16[3584,896]{0,1:T(8,128)(2,1)} %fusion.8) | data formatting | bytes 12845056 | tf_op jit(solution)/shard_map/convert_element_type | solution.py:133
  214.4 129.7 %all-to-all-done.7 = bf16[64,56,896]{2,1,0:T(8,128)(2,1)} async-done(((bf16[64,56,896]{2,1,0:T(8,128)(2,1)}), bf16[64,56,896]{2,1,0:T(8,128)(2,1)}, u32[]{:S(2)}, u32[]{:S(2)}) %all-to-all-start.7) | async-done | bytes 6422560 | tf_op jit(solution)/shard_map/all_to_all | solution.py:138
  344.1 6.0 %all-to-all-start.6 = ((bf16[64,56,896]{2,1,0:T(8,128)(2,1)}), bf16[64,56,896]{2,1,0:T(8,128)(2,1)}, u32[]{:S(2)}, u32[]{:S(2)}) async-start(bf16[64,56,896]{2,1,0:T(8,128)(2,1)} %bitcast.58), calls=%async_computation.6 | async-start | bytes 12845056 | tf_op jit(solution)/shard_map/all_to_all | solution.py:132
  351.7 4.4 convert_reduce_fusion
  356.1 138.0 %all-to-all-done.6 = bf16[64,56,896]{2,1,0:T(8,128)(2,1)} async-done(((bf16[64,56,896]{2,1,0:T(8,128)(2,1)}), bf16[64,56,896]{2,1,0:T(8,128)(2,1)}, u32[]{:S(2)}, u32[]{:S(2)}) %all-to-all-start.6) | async-done | bytes 6422560 | tf_op jit(solution)/shard_map/all_to_all | solution.py:132
  494.1 4.4 convert_reduce_fusion.1
  (76 shorter events, 9.4 us)
Async XLA Ops:
  7.2 61.1 %copy-start = (bf16[2,64,896]{2,1,0:T(8,128)(2,1)S(1)}, bf16[2,64,896]{2,1,0:T(8,128)(2,1)}, u32[]{:S(2)}) copy-start(bf16[2,64,896]{2,1,0:T(8,128)(2,1)} %param.11) | copy-start | bytes 688132
  7.2 59.8 %copy-start.7 = (bf16[896]{0:T(1024)(128)(2,1)S(1)}, bf16[896]{0:T(1024)(128)(2,1)}, u32[]{:S(2)}) copy-start(bf16[896]{0:T(1024)(128)(2,1)} %param.20) | copy-start | bytes 5380
  7.2 59.8 %copy-start.6 = (s32[2]{0:T(128)S(1)}, s32[2]{0:T(128)}, u32[]{:S(2)}) copy-start(s32[2]{0:T(128)} %param.14) | copy-start | bytes 28
  7.2 130.8 %all-gather.2.cloned.1.call-start = ((), (), s32[]{:S(2)}) async-start(), calls=%async_computation.8 | async-start | bytes 26091520 | tf_op jit(solution)/shard_map/all_gather | solution.py:28
  60.1 18.3 %all-to-all-start = ((bf16[4,2,64,896]{3,2,1,0:T(8,128)(2,1)}), bf16[4,2,64,896]{3,2,1,0:T(8,128)(2,1)S(1)}, u32[]{:S(2)}, u32[]{:S(2)}) async-start(bf16[4,2,64,896]{3,2,1,0:T(8,128)(2,1)} %broadcast_in_dim.36), calls=%async_computation | async-start | bytes 1835008 | tf_op jit(solution)/shard_map/all_to_all | solution.py:19
  79.1 74.8 %all-to-all-start.4 = ((f32[64,1,1]{2,1,0:T(1,128)}), f32[64,1,1]{2,1,0:T(1,128)S(1)}, u32[]{:S(2)}, u32[]{:S(2)}) async-start(f32[64,1,1]{2,1,0:T(1,128)} %broadcast_in_dim.42), calls=%async_computation.4 | async-start | bytes 65536 | tf_op jit(solution)/shard_map/all_to_all | solution.py:19
  138.0 12.0 %copy-start.9 = (bf16[3584,3584]{1,0:T(8,128)(2,1)S(1)}, bf16[3584,3584]{1,0:T(8,128)(2,1)}, u32[]{:S(2)}) copy-start(bf16[3584,3584]{1,0:T(8,128)(2,1)} %all-gather.2.cloned.1.call-done) | copy-start | bytes 77070336
  152.0 12.6 %copy-start.8 = (f32[2,64]{1,0:T(2,128)S(1)}, f32[2,64]{1,0:T(2,128)}, u32[]{:S(2)}) copy-start(f32[2,64]{1,0:T(2,128)} %param.12) | copy-start | bytes 1540
  154.5 9.6 %all-to-all-start.3 = ((f32[4,1,640]{2,1,0:T(1,128)}), f32[4,1,640]{2,1,0:T(1,128)S(1)}, u32[]{:S(2)}, u32[]{:S(2)}) async-start(f32[4,1,640]{2,1,0:T(1,128)} %broadcast_in_dim.39), calls=%async_computation.3 | async-start | bytes 20480 | tf_op jit(solution)/shard_map/all_to_all | solution.py:19
  167.8 21.9 %all-to-all-start.5 = ((f32[64,1,898]{2,1,0:T(1,128)}), f32[64,1,898]{2,1,0:T(1,128)S(1)}, u32[]{:S(2)}, u32[]{:S(2)}) async-start(f32[64,1,898]{2,1,0:T(1,128)} %broadcast_in_dim.43), calls=%async_computation.5 | async-start | bytes 524288 | tf_op jit(solution)/shard_map/all_to_all | solution.py:19
  189.7 154.4 %all-to-all-start.7 = ((bf16[64,56,896]{2,1,0:T(8,128)(2,1)}), bf16[64,56,896]{2,1,0:T(8,128)(2,1)}, u32[]{:S(2)}, u32[]{:S(2)}) async-start(bf16[64,56,896]{2,1,0:T(8,128)(2,1)} %bitcast.57), calls=%async_computation.7 | async-start | bytes 12845056 | tf_op jit(solution)/shard_map/all_to_all | solution.py:138
  344.1 6.0 %copy-start.1 = (bf16[56,896]{1,0:T(8,128)(2,1)S(1)}, bf16[56,896]{1,0:T(8,128)(2,1)}, u32[]{:S(2)}) copy-start(bf16[56,896]{1,0:T(8,128)(2,1)} %param.19) | copy-start | bytes 301060
  344.1 6.0 %copy-start.2 = (bf16[56,896]{1,0:T(8,128)(2,1)S(1)}, bf16[56,896]{1,0:T(8,128)(2,1)}, u32[]{:S(2)}) copy-start(bf16[56,896]{1,0:T(8,128)(2,1)} %param.18) | copy-start | bytes 301060
  344.1 6.0 %copy-start.3 = (bf16[56,896]{1,0:T(8,128)(2,1)S(1)}, bf16[56,896]{1,0:T(8,128)(2,1)}, u32[]{:S(2)}) copy-start(bf16[56,896]{1,0:T(8,128)(2,1)} %param.17) | copy-start | bytes 301060
  344.1 6.0 %copy-start.4 = (bf16[56,896]{1,0:T(8,128)(2,1)S(1)}, bf16[56,896]{1,0:T(8,128)(2,1)}, u32[]{:S(2)}) copy-start(bf16[56,896]{1,0:T(8,128)(2,1)} %param.16) | copy-start | bytes 301060
  344.1 149.9 %all-to-all-start.6 = ((bf16[64,56,896]{2,1,0:T(8,128)(2,1)}), bf16[64,56,896]{2,1,0:T(8,128)(2,1)}, u32[]{:S(2)}, u32[]{:S(2)}) async-start(bf16[64,56,896]{2,1,0:T(8,128)(2,1)} %bitcast.58), calls=%async_computation.6 | async-start | bytes 12845056 | tf_op jit(solution)/shard_map/all_to_all | solution.py:132
  351.1 147.4 %copy-start.5 = (f32[898]{0:T(1024)}, f32[898]{0:T(1024)S(1)}, u32[]{:S(2)}) copy-start(f32[898]{0:T(1024)S(1)} %reduce_sum.117) | copy-start | bytes 10780
Sparse Core Ops, SparseCore 0:
  10.7 127.2 all-gather.1
where the time goes:
time: 507 us; the launch traced here: 505 us
  waiting for transfers between devices  333 us (66%)
  blocking collectives  39.2 us (8%)
  starting transfers between devices  37.6 us (7%)
  local copies, waits for them, and re-layouts  33.8 us (7%)
  matrix products  24 us (5%)
  other arithmetic  20.3 us (4%)
  between operations  17.6 us (3%)
    all_to_all x1, waiting for transfers between devices, on_device(): lax.all_to_all(term_one.astype(jnp.bfloat16), 'dp', split_axis=0, concat_...  138 us
    all_to_all x1, waiting for transfers between devices, on_device(): lax.all_to_all(term_two.astype(jnp.bfloat16), 'dp', split_axis=0, concat_...  130 us
    all_gather x1, waiting for transfers between devices, side_by_side(): lax.all_gather(both, axis, axis=dim, tiled=True)  53 us
    all_to_all x4, starting transfers between devices, sent_to_all(): return lax.all_to_all(copies, axis, split_axis=0, concat_axis=0, tiled=True)  21.2 us
    all_to_all x1, blocking collectives, lookup(): lax.all_to_all(requests, 'dp', split_axis=0, concat_axis=0, tiled=True)  20.6 us
    all_to_all x1, blocking collectives, lookup(): lax.all_to_all(found, 'dp', split_axis=0, concat_axis=0, tiled=True)  18.6 us
    dot_general x4, matrix products, add_rows(): jnp.dot(flat, piece, preferred_element_type=jnp.float32)  14.2 us
    all_to_all x4, waiting for transfers between devices, sent_to_all(): return lax.all_to_all(copies, axis, split_axis=0, concat_axis=0, tiled=True)  12.2 us
  transfers between devices with their start and end apart: 7, of which 5 were waited for; matrix products, arithmetic and copies ran while one was open for 13% of the time, Pallas kernels for 0%

commit v1 on v0

v1 whole, which is shorter than its diff:
```python
import jax
import jax.numpy as jnp
from jax import lax
from jax.sharding import Mesh
from jax.sharding import PartitionSpec as P

discount = 0.99
expectile = 0.7
polyak_rate = 0.005

ZS, YS, CS, XS = 8, 4, 2, 4
ROWS = ("z", "y", "c")
f32 = jnp.float32
bf16 = jnp.bfloat16


def exchange(pieces, axes):
    return lax.all_to_all(pieces, axes, split_axis=0, concat_axis=0, tiled=True)


def to_all(shard, axes):
    return exchange(jnp.broadcast_to(shard, (lax.axis_size(axes), *shard.shape)), axes)


def swapped(a):
    return lax.ppermute(a, "c", ((0, 1), (1, 0)))


def head_gelu(inputs):
    return jax.nn.gelu(inputs, approximate=True)


def slope(preact, upstream):
    _, pullback = jax.vjp(head_gelu, preact)
    return pullback(upstream)[0]


def critic_terms(q_first, q_second, t_first, t_second, values, rewards, lengths):
    positions = jnp.arange(values.shape[1], dtype=f32)[None, :]
    valid = positions < lengths[:, None]
    follows = positions + 1 < lengths[:, None]
    shifted = jnp.concatenate([values[:, 1:], jnp.zeros_like(values[:, :1])], axis=1)
    target = rewards + discount * jnp.where(follows, shifted, 0.0)
    lowest = jnp.minimum(t_first, t_second)
    spread = lowest - values
    weights = jnp.where(spread < 0.0, 1.0 - expectile, expectile)
    err_one = q_first - target
    err_two = q_second - target
    loss_sum = jnp.sum(
        jnp.where(valid, err_one * err_one + err_two * err_two + weights * spread * spread, 0.0)
    )
    grad_first = jnp.where(valid, 2.0 * err_one, 0.0)
    grad_second = jnp.where(valid, 2.0 * err_two, 0.0)
    grad_values = jnp.where(valid, -2.0 * weights * spread, 0.0)
    return (grad_first, grad_second, grad_values, loss_sum)


def split_thrice(a):
    first = a.astype(bf16)
    rest = a - first.astype(f32)
    second = rest.astype(bf16)
    third = (rest - second.astype(f32)).astype(bf16)
    return (first, second, third)


def lookup(ids, table):
    count = ids.shape[0]
    local_rows = table.shape[0]
    holders = lax.axis_size(ROWS)
    per_holder = count // holders
    columns = table.shape[1] // YS
    place = jnp.arange(count, dtype=jnp.int32)
    holder = ids // local_rows
    local = ids % local_rows
    earlier = (holder[:, None] == holder[None, :]) & (place[None, :] < place[:, None])
    slot = per_holder * holder + jnp.sum(earlier.astype(jnp.int32), axis=1)
    coded = local + 4096 * place
    asked = jnp.sum(jnp.where(slot[:, None] == place[None, :], coded[:, None], 0), axis=0)
    got = exchange(asked.reshape(holders, per_holder), ROWS).reshape(count)
    found = table[got & 4095]
    where = (got >> 12).astype(bf16)
    found = found.reshape(ZS, YS, CS, per_holder, YS, columns).transpose(0, 4, 2, 1, 3, 5)
    where = jnp.broadcast_to(
        where.reshape(ZS, 1, YS, CS, per_holder, 1).transpose(0, 1, 3, 2, 4, 5),
        (ZS, YS, CS, YS, per_holder, 1),
    )
    sent = jnp.concatenate([found, where], axis=-1).reshape(holders, YS * per_holder, columns + 1)
    back = exchange(sent, ROWS).reshape(holders * YS * per_holder, columns + 1)
    slots = jnp.arange(holders * YS * per_holder, dtype=jnp.int32)
    token = (slots // per_holder % YS) * count + back[:, columns].astype(jnp.int32)
    one_hot = (token[:, None] == jnp.arange(YS * count, dtype=jnp.int32)[None, :]).astype(bf16)
    return lax.dot_general(
        one_hot, back[:, :columns], (((0,), (0,)), ((), ())), preferred_element_type=f32
    ).astype(bf16)


def on_device(
    hidden, rewards, actions, lengths, table, q_one, q_two, t_one, t_two, value_weight, value_bias
):
    prompts, slots, width = hidden.shape
    tokens = prompts * slots
    core = lax.axis_index("c")
    share, head_cols = q_one.shape
    cols = head_cols // YS
    local = hidden.reshape(tokens, width)

    heads = jnp.stack([jnp.stack([q_one, t_one]), jnp.stack([q_two, t_two])])
    pieces = heads.reshape(CS, 2, share, YS, cols).transpose(3, 0, 2, 1, 4)
    pieces = exchange(pieces.reshape(YS * CS, share, 2 * cols), ("y", "c"))
    weights = lax.all_gather(
        pieces.reshape(YS * CS * share, 2 * cols), "z", axis=0, tiled=True
    ).reshape(XS, width, 2 * cols)

    own = to_all(local, ("y", "x")).reshape(YS, XS, tokens, width)
    other = swapped(own)
    embed_own = lookup(actions.reshape(tokens), table)
    embed_other = swapped(embed_own)

    def forward(states):
        return jnp.einsum("yxtk,xkn->ytn", states, weights, preferred_element_type=f32).reshape(
            YS * tokens, 2 * cols
        )

    pre_own, pre_other = forward(own), forward(other)

    def scores(pre, embed):
        e = embed.astype(f32)
        return (
            jnp.sum(head_gelu(pre[:, :cols]) * e, axis=1).reshape(YS, tokens),
            jnp.sum(head_gelu(pre[:, cols:]) * e, axis=1).reshape(YS, tokens),
        )

    q_own, t_own = scores(pre_own, embed_own)
    q_other, t_other = scores(pre_other, embed_other)
    value_part = jnp.dot(local, value_weight, preferred_element_type=f32)

    def by_core(a, b):
        return jnp.where(core == 0, jnp.stack([a, b]), jnp.stack([b, a]))

    message = jnp.concatenate(
        [
            by_core(q_own, q_other).reshape(-1),
            by_core(t_own, t_other).reshape(-1),
            value_part,
            rewards.reshape(-1),
            jnp.repeat(lengths.astype(f32), slots),
        ]
    ).reshape(-1, tokens)
    said = to_all(message, ("y", "c", "x")).reshape(YS, CS, XS, -1, tokens)
    summed = jnp.sum(said[..., : 4 * CS * YS, :], axis=(0, 2))
    group = CS * YS
    q_first, q_second = summed[0, :group], summed[1, :group]
    t_first, t_second = summed[0, group : 2 * group], summed[1, group : 2 * group]

    def by_place(a):
        return a.transpose(1, 0, 2).reshape(group, tokens)

    values = by_place(jnp.sum(said[..., 2 * group, :], axis=2)) + value_bias[0]
    all_rewards = by_place(said[:, :, 0, 2 * group + 1, :])
    all_lengths = by_place(said[:, :, 0, 2 * group + 2, :])

    def prompts_of(a):
        return a.reshape(group * prompts, slots)

    grad_first, grad_second, grad_values, loss_sum = critic_terms(
        prompts_of(q_first),
        prompts_of(q_second),
        prompts_of(t_first),
        prompts_of(t_second),
        prompts_of(values),
        prompts_of(all_rewards),
        prompts_of(all_lengths)[:, 0],
    )
    my_grad = jnp.where(core == 0, grad_first, grad_second).reshape(CS, -1)
    grad_values = grad_values.reshape(CS, -1)

    def own_and_other(a):
        return jnp.where(core == 0, a[0], a[1]), jnp.where(core == 0, a[1], a[0])

    g_own, g_other = own_and_other(my_grad)
    e_own, e_other = own_and_other(grad_values)

    def back(pre, embed, g, e):
        d = slope(pre[:, :cols], g[:, None] * embed.astype(f32)).astype(bf16)
        return jnp.concatenate([d, jnp.stack(split_thrice(e), axis=1)], axis=1).reshape(
            YS, tokens, cols + 3
        )

    def against(states, d):
        return jnp.einsum("yxtk,ytn->xkn", states, d, preferred_element_type=f32)

    grads = against(own, back(pre_own, embed_own, g_own, e_own)) + against(
        other, back(pre_other, embed_other, g_other, e_other)
    )
    group_count = jnp.sum(prompts_of(all_lengths)[:, 0])
    terms = grads[..., :cols].astype(bf16).reshape(ZS * YS * CS, share, cols)
    value_terms = jnp.sum(
        lax.dynamic_index_in_dim(grads[..., cols:], lax.axis_index("x"), 0, keepdims=False), axis=1
    )
    totals = jnp.concatenate(
        [value_terms, jnp.stack([jnp.sum(grad_values), loss_sum, group_count])]
    )
    totals = jnp.sum(to_all(totals, "z"), axis=0)
    factor = 1.0 / totals[width + 2]
    value_grad = totals[:width] * factor
    bias_grad = totals[width] * factor
    loss_total = totals[width + 1] * factor

    landed = exchange(terms, ROWS).reshape(ZS, YS, CS, share, cols)
    head_grads = jnp.sum(landed.astype(f32), axis=0) * factor
    head_grads = head_grads.transpose(1, 2, 0, 3).reshape(CS, share, head_cols)

    new_one = (
        (1.0 - polyak_rate) * t_one.astype(f32) + polyak_rate * q_one.astype(f32)
    ).astype(bf16)
    new_two = (
        (1.0 - polyak_rate) * t_two.astype(f32) + polyak_rate * q_two.astype(f32)
    ).astype(bf16)
    return (
        loss_total,
        head_grads[0],
        head_grads[1],
        value_grad,
        bias_grad.reshape(1),
        new_one,
        new_two,
    )


def solution(mesh):
    fine = Mesh(mesh.devices.reshape(ZS, YS, CS, XS), ("z", "y", "c", "x"))
    in_specs = (
        P(ROWS, None, "x"),
        P(ROWS, None),
        P(ROWS, None),
        P(ROWS),
        P(ROWS, "x"),
        P(ROWS, "x"),
        P(ROWS, "x"),
        P(ROWS, "x"),
        P(ROWS, "x"),
        P("x"),
        P(),
    )
    out_specs = (P(), P(ROWS, "x"), P(ROWS, "x"), P("x"), P(), P(ROWS, "x"), P(ROWS, "x"))
    return jax.shard_map(
        on_device, mesh=fine, in_specs=in_specs, out_specs=out_specs, check_vma=False
    )
```

time: 507 us -> 252 us (0.50)
  waiting for transfers between devices: 333 us -> 118 us
  other arithmetic: 20.3 us -> 9.08 us
  starting transfers between devices: 37.6 us -> 28.3 us
  local copies, waits for them, and re-layouts: 33.8 us -> 25.4 us
  matrix products: 24 us -> 16.8 us
  blocking collectives: 39.2 us -> 34 us
    all_to_all x6 -> x5, waiting for transfers between devices: 280 us -> 117 us  [exchange(): return lax.all_to_all(pieces, axes, split_axis=0, concat_axis=0, tiled=True)]
    all_gather x1, waiting for transfers between devices: 53 us -> 0.02 us  [on_device(): lax.all_gather(pieces.reshape(YS * CS * share, 2 * cols), 'z', axis=0, ti...]
    convert_element_type x2 -> x1, local copies, waits for them, and re-layouts: 19 us -> 0.13 us  [lookup(): where = (got >> 12).astype(bf16)]
    all_to_all x6 -> x5, starting transfers between devices: 37.6 us -> 28 us  [exchange(): return lax.all_to_all(pieces, axes, split_axis=0, concat_axis=0, tiled=True)]
    reduce_sum x6 -> x9, other arithmetic: 10.4 us -> 1.78 us  [the longest x1 0.64 us: on_device(): jnp.sum(grad_values)]
    dot_general x8 -> x6, matrix products: 24 us -> 16.8 us  [the longest x2 9.72 us: forward(): jnp.einsum('yxtk,xkn->ytn', states, weights, preferred_element_type=f32)]
    slice x1 -> x9, local copies, waits for them, and re-layouts: 0.58 us -> 5.86 us  [the longest x2 4.94 us: on_device(): terms = grads[..., :cols].astype(bf16).reshape(ZS * YS * CS, share, cols)]
    another operation x0 -> x12, local copies, waits for them, and re-layouts: none -> 5.19 us  [the longest x8 4.9 us: on_device(): heads = jnp.stack([jnp.stack([q_one, t_one]), jnp.stack([q_two, t_two])])]
  transfers between devices with their start and end apart: 7 -> 8, of which waited for: 5 -> 5; matrix products, arithmetic and copies ran while one was open for 13% -> 10% of each run, Pallas kernels for 0% -> 0%
where the time goes in v1:
time: 252 us; the launch traced here: 251 us
  waiting for transfers between devices  118 us (47%)
  blocking collectives  34 us (13%)
  starting transfers between devices  28.3 us (11%)
  local copies, waits for them, and re-layouts  25.4 us (10%)
  between operations  19.5 us (8%)
  matrix products  16.8 us (7%)
  other arithmetic  9.08 us (4%)
    all_to_all x5, waiting for transfers between devices, exchange(): return lax.all_to_all(pieces, axes, split_axis=0, concat_axis=0, tiled=True)  117 us
    all_to_all x2, blocking collectives, exchange(): return lax.all_to_all(pieces, axes, split_axis=0, concat_axis=0, tiled=True)  34 us
    all_to_all x5, starting transfers between devices, exchange(): return lax.all_to_all(pieces, axes, split_axis=0, concat_axis=0, tiled=True)  28 us
    dot_general x2, matrix products, forward(): jnp.einsum('yxtk,xkn->ytn', states, weights, preferred_element_type=f32)  9.72 us
    dot_general x2, matrix products, against(): return jnp.einsum('yxtk,ytn->xkn', states, d, preferred_element_type=f32)  6.19 us
  transfers between devices with their start and end apart: 8, of which 5 were waited for; matrix products, arithmetic and copies ran while one was open for 10% of the time, Pallas kernels for 0%

profile of v1, /device:TPU:8, one launch (start us, length us, event | category | flops | bytes accessed | tf_op | source)
XLA Modules:
  0.0 251.1 jit_solution(15188714462729160303)
XLA Ops:
  7.2 1.1 stack.50
  8.4 1.0 stack.51
  9.7 1.0 stack.53
  10.9 1.0 stack.54
  12.1 1.1 maximum_bitcast_fusion
  13.6 13.4 %all_to_all.40 = bf16[8,56,448]{2,1,0:T(8,128)(2,1)} all-to-all(bf16[8,56,448]{2,1,0:T(8,128)(2,1)S(1)} %reshape.501), channel_id=1, replica_groups=mesh['z'=8,'y'=4,'c'=2,'x'=4] {'y','c'}, dimensions={0} | all-to-all | bytes 802816 | tf_op jit(solution)/shard_map/all_to_all | solution.py:18
  26.9 2.3 broadcast_in_dim.66
  29.3 6.1 %all-to-all-start.1 = ((bf16[16,128,896]{2,1,0:T(8,128)(2,1)}), bf16[16,128,896]{2,1,0:T(8,128)(2,1)}, u32[]{:S(2)}, u32[]{:S(2)}) async-start(bf16[16,128,896]{2,1,0:T(8,128)(2,1)} %broadcast_in_dim.66), calls=%async_computation.1 | async-start | bytes 7340032 | tf_op jit(solution)/shard_map/all_to_all | solution.py:18
  36.2 52.3 %all-to-all-done.1 = bf16[16,128,896]{2,1,0:T(8,128)(2,1)} async-done(((bf16[16,128,896]{2,1,0:T(8,128)(2,1)}), bf16[16,128,896]{2,1,0:T(8,128)(2,1)}, u32[]{:S(2)}, u32[]{:S(2)}) %all-to-all-start.1) | async-done | bytes 3670048 | tf_op jit(solution)/shard_map/all_to_all | solution.py:18
  89.2 20.6 %all_to_all.41 = s32[64,1,2]{2,1,0:T(1,128)S(1)} all-to-all(s32[64,1,2]{2,1,0:T(1,128)S(1)} %bitcast.131), channel_id=1, replica_groups=mesh['z'=8,'y'=4,'c'=2,'x'=4] {'z','y','c'}, dimensions={0} | all-to-all | bytes 1024 | tf_op jit(solution)/shard_map/all_to_all | solution.py:18
  110.1 3.8 %gather_fusion = bf16[128,896]{1,0:T(8,128)(2,1)S(1)} fusion(bf16[2376,896]{1,0:T(8,128)(2,1)} %param.15, s32[1024]{0:T(1024)S(1)} %pad_clamp_fusion), kind=kCustom, calls=%fused_computation | custom fusion | bytes 459264 | tf_op jit(solution)/shard_map/gather | solution.py:80
  115.5 0.9 reshape.508
  116.5 5.5 %all-to-all-start.3 = ((bf16[64,8,225]{2,1,0:T(8,128)(2,1)}), bf16[64,8,225]{2,1,0:T(8,128)(2,1)S(1)}, u32[]{:S(2)}, u32[]{:S(2)}) async-start(bf16[64,8,225]{2,1,0:T(8,128)(2,1)} %reshape.508), calls=%async_computation.3 | async-start | bytes 524288 | tf_op jit(solution)/shard_map/all_to_all | solution.py:18
  122.4 11.9 %all-to-all-done.3 = bf16[64,8,225]{2,1,0:T(8,128)(2,1)S(1)} async-done(((bf16[64,8,225]{2,1,0:T(8,128)(2,1)}), bf16[64,8,225]{2,1,0:T(8,128)(2,1)S(1)}, u32[]{:S(2)}, u32[]{:S(2)}) %all-to-all-start.3) | async-done | bytes 230432 | tf_op jit(solution)/shard_map/all_to_all | solution.py:18
  134.6 5.4 %convolution_bitcast_fusion.1 = f32[4,56,8,128]{3,2,1,0:T(8,128)S(1)} fusion(bf16[4,896,448,1]{2,1,0,3:T(8,128)(2,1)} %bitcast.144, bf16[4,4,128,896]{3,2,1,0:T(8,128)(2,1)} %bitcast.5), kind=kOutput, calls=%fused_computation.6 | convolution fusion | flops 1644167168 | bytes 7798784 | tf_op jit(solution)/shard_map/yxtk,xkn->ytn/dot_general | solution.py:120
  141.1 0.9 copy-done.7
  142.1 4.3 %convolution_bitcast_fusion = f32[4,56,8,128]{3,2,1,0:T(8,128)S(1)} fusion(bf16[4,896,448,1]{2,1,0,3:T(8,128)(2,1)S(1)} %bitcast.145, bf16[4,4,128,896]{3,2,1,0:T(8,128)(2,1)} %collective-permute-done), kind=kOutput, calls=%fused_computation.5 | convolution fusion | flops 1644167168 | bytes 7798784 | tf_op jit(solution)/shard_map/yxtk,xkn->ytn/dot_general | solution.py:120
  146.9 0.8 broadcast_in_dim.72
  147.7 6.1 %all-to-all-start.4 = ((f32[32,19,128]{2,1,0:T(8,128)}), f32[32,19,128]{2,1,0:T(8,128)S(1)}, u32[]{:S(2)}, u32[]{:S(2)}) async-start(f32[32,19,128]{2,1,0:T(8,128)} %broadcast_in_dim.72), calls=%async_computation.4 | async-start | bytes 786432 | tf_op jit(solution)/shard_map/all_to_all | solution.py:18
  154.5 8.5 %all-to-all-done.4 = f32[32,19,128]{2,1,0:T(8,128)S(1)} async-done(((f32[32,19,128]{2,1,0:T(8,128)}), f32[32,19,128]{2,1,0:T(8,128)S(1)}, u32[]{:S(2)}, u32[]{:S(2)}) %all-to-all-start.4) | async-done | bytes 311328 | tf_op jit(solution)/shard_map/all_to_all | solution.py:18
  166.6 3.1 %fusion.46 = f32[227,4,896,1]{2,0,1,3:T(8,128)S(1)} fusion(bf16[4,4,128,896]{3,2,1,0:T(8,128)(2,1)} %bitcast.5, bf16[4,128,1]{1,2,0:T(2,128)(2,1)S(1)} %get-tuple-element.35, bf16[4,128,1]{1,2,0:T(2,128)(2,1)S(1)} %get-tuple-element.36, bf16[4,128,1]{1,2,0:T(2,128)(2,1)S(1)} %get-tuple-element.34, bf16[4,128,224]{1,2,0:T(8,128)(2,1)S(1)} %copy_bitcast_fusion.4), kind=kOutput, calls=%fused_computation.73 | convolution fusion | flops 834023424 | bytes 7156736 | tf_op jit(solution)/shard_map/yxtk,ytn->xkn/dot_general | solution.py:190
  170.0 3.1 %fusion = f32[4,896,227]{1,2,0:T(8,128)S(1)} fusion(f32[227,4,896,1]{2,0,1,3:T(8,128)S(1)} %fusion.46, bf16[4,4,128,896]{3,2,1,0:T(8,128)(2,1)} %collective-permute-done, bf16[4,128,1]{1,2,0:T(2,128)(2,1)S(1)} %get-tuple-element.32, bf16[4,128,1]{1,2,0:T(2,128)(2,1)S(1)} %get-tuple-element.33, bf16[4,128,1]{1,2,0:T(2,128)(2,1)S(1)} %get-tuple-element.31, ...), kind=kOutput, calls=%fused_computation.3 | convolution fusion | flops 834836992 | bytes 10411008 | tf_op jit(solution)/shard_map/yxtk,ytn->xkn/dot_general | solution.py:190
  173.2 2.0 pad_maximum_fusion.1
  175.9 3.3 %all-to-all-start.5 = ((f32[8,1,899]{2,1,0:T(1,128)}), f32[8,1,899]{2,1,0:T(1,128)S(1)}, u32[]{:S(2)}, u32[]{:S(2)}) async-start(f32[8,1,899]{2,1,0:T(1,128)} %broadcast_in_dim.79), calls=%async_computation.5 | async-start | bytes 65536 | tf_op jit(solution)/shard_map/all_to_all | solution.py:18
  179.2 1.3 slice.194
  180.6 3.6 %copy.202 = bf16[4,896,224]{2,1,0:T(8,128)(2,1)} copy(bf16[4,896,224]{1,2,0:T(8,128)(2,1)} %slice.194) | data formatting | bytes 3211264 | tf_op jit(solution)/shard_map/slice | solution.py:196
  184.2 3.0 %all-to-all-done.5 = f32[8,1,899]{2,1,0:T(1,128)S(1)} async-done(((f32[8,1,899]{2,1,0:T(1,128)}), f32[8,1,899]{2,1,0:T(1,128)S(1)}, u32[]{:S(2)}, u32[]{:S(2)}) %all-to-all-start.5) | async-done | bytes 28800 | tf_op jit(solution)/shard_map/all_to_all | solution.py:18
  187.2 6.9 %all-to-all-start.6 = ((bf16[64,56,224]{2,1,0:T(8,128)(2,1)}), bf16[64,56,224]{2,1,0:T(8,128)(2,1)S(1)}, u32[]{:S(2)}, u32[]{:S(2)}) async-start(bf16[64,56,224]{2,1,0:T(8,128)(2,1)} %bitcast.48), calls=%async_computation.6 | async-start | bytes 3670016 | tf_op jit(solution)/shard_map/all_to_all | solution.py:18
  194.1 0.8 add_convert_fusion
  198.1 41.6 %all-to-all-done.6 = bf16[64,56,224]{2,1,0:T(8,128)(2,1)S(1)} async-done(((bf16[64,56,224]{2,1,0:T(8,128)(2,1)}), bf16[64,56,224]{2,1,0:T(8,128)(2,1)S(1)}, u32[]{:S(2)}, u32[]{:S(2)}) %all-to-all-start.6) | async-done | bytes 1605664 | tf_op jit(solution)/shard_map/all_to_all | solution.py:18
  240.2 0.9 squeeze.20
  241.1 0.9 squeeze.40
  (115 shorter events, 12.9 us)
Async XLA Ops:
  7.2 19.8 %copy-start = (bf16[2,64,896]{2,1,0:T(8,128)(2,1)S(1)}, bf16[2,64,896]{2,1,0:T(8,128)(2,1)}, u32[]{:S(2)}) copy-start(bf16[2,64,896]{2,1,0:T(8,128)(2,1)} %param.11) | copy-start | bytes 688132
  29.3 59.2 %copy-start.6 = (s32[2,64]{1,0:T(2,128)S(1)}, s32[2,64]{1,0:T(2,128)}, u32[]{:S(2)}) copy-start(s32[2,64]{1,0:T(2,128)} %param.13) | copy-start | bytes 1540
  29.3 59.2 %all-to-all-start.1 = ((bf16[16,128,896]{2,1,0:T(8,128)(2,1)}), bf16[16,128,896]{2,1,0:T(8,128)(2,1)}, u32[]{:S(2)}, u32[]{:S(2)}) async-start(bf16[16,128,896]{2,1,0:T(8,128)(2,1)} %broadcast_in_dim.66), calls=%async_computation.1 | async-start | bytes 7340032 | tf_op jit(solution)/shard_map/all_to_all | solution.py:18
  35.4 86.6 %copy-start.5 = (bf16[896]{0:T(1024)(128)(2,1)S(1)}, bf16[896]{0:T(1024)(128)(2,1)}, u32[]{:S(2)}) copy-start(bf16[896]{0:T(1024)(128)(2,1)} %param.20) | copy-start | bytes 5380
  35.4 86.6 %copy-start.8 = (f32[2,64]{1,0:T(2,128)S(1)}, f32[2,64]{1,0:T(2,128)}, u32[]{:S(2)}) copy-start(f32[2,64]{1,0:T(2,128)} %param.12) | copy-start | bytes 1540
  35.4 86.7 %copy-start.9 = (s32[2]{0:T(128)S(1)}, s32[2]{0:T(128)}, u32[]{:S(2)}) copy-start(s32[2]{0:T(128)} %param.14) | copy-start | bytes 28
  35.4 99.2 %all-gather.2.cloned.1.call-start = ((), (), s32[]{:S(2)}) async-start(), calls=%async_computation.7 | async-start | bytes 4128768 | tf_op jit(solution)/shard_map/all_gather | solution.py:110
  88.5 52.6 %collective-permute-start = (bf16[4,4,128,896]{3,2,1,0:T(8,128)(2,1)}, bf16[4,4,128,896]{3,2,1,0:T(8,128)(2,1)}, u32[]{:S(2)}, u32[]{:S(2)}) collective-permute-start(bf16[4,4,128,896]{3,2,1,0:T(8,128)(2,1)} %bitcast.5), channel_id=1, source_target_pairs={{0,4},{4,0},{1,5},{5,1},{2,6},{6,2},{3,7},{7,3},{8,12},{12,8},{9,1... | collective-permute-start | bytes 11010056 | tf_op jit(solution)/shard_map/ppermute | solution.py:26
  116.5 17.8 %all-to-all-start.3 = ((bf16[64,8,225]{2,1,0:T(8,128)(2,1)}), bf16[64,8,225]{2,1,0:T(8,128)(2,1)S(1)}, u32[]{:S(2)}, u32[]{:S(2)}) async-start(bf16[64,8,225]{2,1,0:T(8,128)(2,1)} %reshape.508), calls=%async_computation.3 | async-start | bytes 524288 | tf_op jit(solution)/shard_map/all_to_all | solution.py:18
  140.0 2.0 copy-start.7
  140.8 5.7 %collective-permute-start.1 = (bf16[512,224]{0,1:T(8,128)(2,1)S(1)}, bf16[512,224]{0,1:T(8,128)(2,1)S(1)}, u32[]{:S(2)}, u32[]{:S(2)}) collective-permute-start(bf16[512,224]{0,1:T(8,128)(2,1)S(1)} %get-tuple-element.41), channel_id=1, source_target_pairs={{0,4},{4,0},{1,5},{5,1},{2,6},{6,2},{3,7},{7,3},{8,12},{12,8},{9,1... | collective-permute-start | bytes 688136 | tf_op jit(solution)/shard_map/ppermute | solution.py:26
  147.7 15.3 %all-to-all-start.4 = ((f32[32,19,128]{2,1,0:T(8,128)}), f32[32,19,128]{2,1,0:T(8,128)S(1)}, u32[]{:S(2)}, u32[]{:S(2)}) async-start(f32[32,19,128]{2,1,0:T(8,128)} %broadcast_in_dim.72), calls=%async_computation.4 | async-start | bytes 786432 | tf_op jit(solution)/shard_map/all_to_all | solution.py:18
  175.9 11.3 %all-to-all-start.5 = ((f32[8,1,899]{2,1,0:T(1,128)}), f32[8,1,899]{2,1,0:T(1,128)S(1)}, u32[]{:S(2)}, u32[]{:S(2)}) async-start(f32[8,1,899]{2,1,0:T(1,128)} %broadcast_in_dim.79), calls=%async_computation.5 | async-start | bytes 65536 | tf_op jit(solution)/shard_map/all_to_all | solution.py:18
  180.5 13.5 %copy-start.1 = (bf16[56,896]{1,0:T(8,128)(2,1)S(1)}, bf16[56,896]{1,0:T(8,128)(2,1)}, u32[]{:S(2)}) copy-start(bf16[56,896]{1,0:T(8,128)(2,1)} %param.19) | copy-start | bytes 301060
  180.5 13.5 %copy-start.2 = (bf16[56,896]{1,0:T(8,128)(2,1)S(1)}, bf16[56,896]{1,0:T(8,128)(2,1)}, u32[]{:S(2)}) copy-start(bf16[56,896]{1,0:T(8,128)(2,1)} %param.17) | copy-start | bytes 301060
  180.5 13.5 %copy-start.3 = (bf16[56,896]{1,0:T(8,128)(2,1)S(1)}, bf16[56,896]{1,0:T(8,128)(2,1)}, u32[]{:S(2)}) copy-start(bf16[56,896]{1,0:T(8,128)(2,1)} %param.18) | copy-start | bytes 301060
  180.5 13.6 %copy-start.4 = (bf16[56,896]{1,0:T(8,128)(2,1)S(1)}, bf16[56,896]{1,0:T(8,128)(2,1)}, u32[]{:S(2)}) copy-start(bf16[56,896]{1,0:T(8,128)(2,1)} %param.16) | copy-start | bytes 301060
  187.2 52.5 %all-to-all-start.6 = ((bf16[64,56,224]{2,1,0:T(8,128)(2,1)}), bf16[64,56,224]{2,1,0:T(8,128)(2,1)S(1)}, u32[]{:S(2)}, u32[]{:S(2)}) async-start(bf16[64,56,224]{2,1,0:T(8,128)(2,1)} %bitcast.48), calls=%async_computation.6 | async-start | bytes 3670016 | tf_op jit(solution)/shard_map/all_to_all | solution.py:18
Sparse Core Ops, SparseCore 0:
  38.0 52.5 all-gather.1
